TPU v7x, 32 devices: a 4x4x1 block of a 4x4x8 slice. The times are simulated.
32 devices in a mesh: dp: 1 (over z), col: 4 (over y), row: 8 (over x, core).
Axes of the slice: x: 4, y: 4, z: 1, core: 2. Of those that a mesh axis runs over, the one named last changes fastest.
The devices are a block of a 4x4x8 slice.
Arguments:
- x_norm: bfloat16 [4096, 2048], P(('dp', 'row'), 'col')
- grad_y: bfloat16 [4096, 2048], P(('dp', 'row'), 'col')
- w_gate: bfloat16 [2048, 16384], P('row', 'col')
- w_up: bfloat16 [2048, 16384], P('row', 'col')
- w_out: bfloat16 [16384, 2048], P('row', 'col')
Outputs:
- output 1: bfloat16 [4096, 2048], P(('dp', 'row'), 'col')
- output 2: float32 [2048, 16384], P(('dp', 'row'), 'col')
- output 3: float32 [2048, 16384], P(('dp', 'row'), 'col')
- output 4: float32 [16384, 2048], P(('dp', 'row'), 'col')
All inputs are finite; a program needn't handle non-finite values.
Results may differ from a plain program's by a relative error of at most 0.0087411.
Values are sent between devices in bfloat16 or wider.
A program may use at most 768 MiB of HBM per device.

v0:
```python
import math
import jax
import jax.numpy as jnp
from jax import lax
from jax.sharding import PartitionSpec as P

GELU_SCALE = math.sqrt(2.0 / math.pi)
ROW_DIMS = (((1,), (1,)), ((), ()))
COL_DIMS = (((0,), (0,)), ((), ()))


def gelu_pair(pre_act):
    pre_f32 = pre_act.astype(jnp.float32)
    inner_arg = GELU_SCALE * (pre_f32 + 0.044715 * pre_f32 * pre_f32 * pre_f32)
    tanh_val = jnp.tanh(inner_arg)
    gelu_val = 0.5 * pre_f32 * (1.0 + tanh_val)
    gelu_der = 0.5 * (1.0 + tanh_val) + 0.5 * pre_f32 * (1.0 - tanh_val * tanh_val) * GELU_SCALE * (1.0 + 3.0 * 0.044715 * pre_f32 * pre_f32)
    return gelu_val, gelu_der


def solution(mesh):
    act_spec = P(("dp", "row"), "col")
    weight_spec = P("row", "col")

    def block_backward(x_blk, gy_blk, gate_blk, up_blk, out_blk):
        x_band = lax.all_gather(x_blk, "col", axis=1, tiled=True)
        gate_band = lax.all_gather(gate_blk, "row", axis=0, tiled=True)
        up_band = lax.all_gather(up_blk, "row", axis=0, tiled=True)
        out_band = lax.all_gather(out_blk, "row", axis=0, tiled=True)
        pre_gate = jnp.dot(x_band, gate_band, preferred_element_type=jnp.float32).astype(jnp.bfloat16)
        pre_up = jnp.dot(x_band, up_band, preferred_element_type=jnp.float32).astype(jnp.bfloat16)
        gelu_val, gelu_der = gelu_pair(pre_gate)
        up_f32 = pre_up.astype(jnp.float32)
        hidden = (gelu_val * up_f32).astype(jnp.bfloat16)
        grad_h_part = lax.dot_general(gy_blk, out_band, ROW_DIMS, preferred_element_type=jnp.float32)
        grad_h = lax.psum_scatter(grad_h_part, "col", scatter_dimension=1, tiled=True)
        hidden_band = lax.all_gather(hidden, "col", axis=1, tiled=True)
        dw_out_part = lax.dot_general(hidden_band, gy_blk, COL_DIMS, preferred_element_type=jnp.float32)
        dw_out = lax.psum_scatter(dw_out_part, "row", scatter_dimension=0, tiled=True)
        grad_gate = (grad_h * up_f32 * gelu_der).astype(jnp.bfloat16)
        grad_up = (grad_h * gelu_val).astype(jnp.bfloat16)
        grad_x_part = lax.dot_general(grad_gate, gate_band, ROW_DIMS, preferred_element_type=jnp.float32) + lax.dot_general(grad_up, up_band, ROW_DIMS, preferred_element_type=jnp.float32)
        grad_x = lax.psum_scatter(grad_x_part, "col", scatter_dimension=1, tiled=True).astype(jnp.bfloat16)
        dw_gate = lax.psum_scatter(lax.dot_general(x_band, grad_gate, COL_DIMS, preferred_element_type=jnp.float32), "row", scatter_dimension=0, tiled=True)
        dw_up = lax.psum_scatter(lax.dot_general(x_band, grad_up, COL_DIMS, preferred_element_type=jnp.float32), "row", scatter_dimension=0, tiled=True)
        return grad_x, dw_gate, dw_up, dw_out

    return jax.shard_map(block_backward, mesh=mesh, in_specs=(act_spec, act_spec, weight_spec, weight_spec, weight_spec), out_specs=(act_spec, act_spec, act_spec, act_spec), check_vma=False)
```

profile of v0, /device:TPU:97, one launch (start us, length us, event | category | flops | bytes accessed | tf_op | source)
XLA Modules:
  0.0 1316.7 jit_solution(17658251132658347713)
XLA Ops:
  7.2 0.0 copy-start
  7.2 0.1 all-gather.6.cloned.1.call-start
  7.3 0.7 all-gather.6.cloned.1.call-update
  8.0 0.1 all-gather.8.cloned.1.call-start
  8.1 0.7 all-gather.8.cloned.1.call-update
  8.8 0.1 all-gather.12.cloned.1.call-start
  8.9 0.7 all-gather.12.cloned.1.call-update
  9.6 0.1 all-gather.10.cloned.1.call-start
  9.7 0.6 all-gather.10.cloned.1.call-update
  10.2 0.1 reduce-scatter.6.cloned.1.call-start
  10.3 86.3 %all-gather.6.cloned.1.call-done = bf16[16384,512]{1,0:T(8,128)(2,1)} async-done(((bf16[2048,512]{1,0:T(8,128)(2,1)}), bf16[16384,512]{1,0:T(8,128)(2,1)}) %all-gather.6.cloned.1.call-update) | async-done | bytes 16777232 | tf_op jit(solution)/shard_map/all_gather | solution.py:29
  96.6 0.0 copy-done
  96.6 23.1 %fusion.11 = f32[512,16384]{1,0:T(8,128)} fusion(bf16[512,512]{1,0:T(8,128)(2,1)S(1)} %copy-done, bf16[16384,512]{1,0:T(8,128)(2,1)} %all-gather.6.cloned.1.call-done), kind=kOutput, calls=%fused_computation.26 | convolution fusion | flops 8589934592 | bytes 50855936 | tf_op jit(solution)/shard_map/dot_general | solution.py:35
  119.7 0.1 reduce-scatter.6.cloned.1.call-update
  119.8 0.4 all-gather.14.cloned.1.call-start
  120.1 6.0 all-gather.8.cloned.1.call-done
  126.2 0.0 copy-start.1
  126.2 84.9 %all-gather.12.cloned.1.call-done = bf16[2048,4096]{1,0:T(8,128)(2,1)} async-done(((bf16[256,4096]{1,0:T(8,128)(2,1)}), bf16[2048,4096]{1,0:T(8,128)(2,1)}) %all-gather.12.cloned.1.call-update) | async-done | bytes 16777232 | tf_op jit(solution)/shard_map/all_gather | solution.py:27
  211.0 14.3 %convolution_convert_fusion = bf16[512,4096]{1,0:T(8,128)(2,1)} fusion(bf16[512,2048]{1,0:T(8,128)(2,1)} %all-gather.8.cloned.1.call-done, bf16[2048,4096]{1,0:T(8,128)(2,1)} %all-gather.12.cloned.1.call-done), kind=kOutput, calls=%fused_computation.23 | convolution fusion | flops 8592031744 | bytes 23068672 | tf_op jit(solution)/shard_map/dot_general | solution.py:30
  225.3 70.4 %all-gather.10.cloned.1.call-done = bf16[2048,4096]{1,0:T(8,128)(2,1)} async-done(((bf16[256,4096]{1,0:T(8,128)(2,1)}), bf16[2048,4096]{1,0:T(8,128)(2,1)}) %all-gather.10.cloned.1.call-update) | async-done | bytes 16777232 | tf_op jit(solution)/shard_map/all_gather | solution.py:28
  295.7 282.5 %reduce-scatter.6.cloned.1.call-done = f32[512,4096]{1,0:T(8,128)} async-done(((f32[512,16384]{1,0:T(8,128)}), f32[512,4096]{1,0:T(8,128)}) %reduce-scatter.6.cloned.1.call-update) | async-done | bytes 8388624 | tf_op jit(solution)/shard_map/reduce_scatter | solution.py:36
  578.2 0.0 copy-done.1
  578.2 21.3 %fusion.7 = (bf16[512,4096]{1,0:T(8,128)(2,1)}, bf16[512,4096]{1,0:T(8,128)(2,1)}) fusion(bf16[512,4096]{1,0:T(8,128)(2,1)} %convolution_convert_fusion, f32[512,4096]{1,0:T(8,128)} %reduce-scatter.6.cloned.1.call-done, bf16[512,2048]{1,0:T(8,128)(2,1)S(1)} %copy-done.1, bf16[2048,4096]{1,0:T(8,128)(2,1)} %all-gather.10.cloned.1.call-done), kind=kOutput, calls=%fused_computation.18 | convolution fusion | flops 8644460544 | bytes 39845888 | tf_op jit(solution)/shard_map/dot_general | solution.py:31
  599.4 0.1 all-gather.14.cloned.1.call-update
  599.5 0.6 reduce-scatter.8.cloned.1.call-start
  600.1 15.1 %fusion.12 = f32[512,2048]{1,0:T(8,128)} fusion(bf16[512,4096]{1,0:T(8,128)(2,1)} %get-tuple-element.9, bf16[2048,4096]{1,0:T(8,128)(2,1)} %all-gather.12.cloned.1.call-done), kind=kOutput, calls=%fused_computation.27 | convolution fusion | flops 8589934592 | bytes 25165824 | tf_op jit(solution)/shard_map/dot_general | solution.py:42
  615.2 20.3 %convolution_add_fusion = f32[512,2048]{1,0:T(8,128)} fusion(f32[512,2048]{1,0:T(8,128)} %fusion.12, bf16[2048,4096]{1,0:T(8,128)(2,1)} %all-gather.10.cloned.1.call-done, f32[512,4096]{1,0:T(8,128)} %reduce-scatter.6.cloned.1.call-done, bf16[512,4096]{1,0:T(8,128)(2,1)} %convolution_convert_fusion), kind=kOutput, calls=%fused_computation.25 | convolution fusion | flops 8614051840 | bytes 37748736 | tf_op jit(solution)/shard_map/dot_general | solution.py:42
  635.5 0.1 reduce-scatter.8.cloned.1.call-update
  635.5 0.2 reduce-scatter.10.cloned.1.call-start
  635.8 17.7 %convolution_bitcast_fusion.1 = f32[2048,4096]{0,1:T(8,128)} fusion(bf16[512,4096]{1,0:T(8,128)(2,1)} %get-tuple-element.9, bf16[512,2048]{1,0:T(8,128)(2,1)S(1)} %copy-done.1), kind=kOutput, calls=%fused_computation.8 | convolution fusion | flops 8589934592 | bytes 39845888 | tf_op jit(solution)/shard_map/dot_general | solution.py:44
  653.4 0.1 reduce-scatter.10.cloned.1.call-update
  653.5 0.1 reduce-scatter.12.cloned.1.call-start
  653.6 24.4 %convolution_bitcast_fusion = f32[2048,4096]{0,1:T(8,128)} fusion(bf16[512,2048]{1,0:T(8,128)(2,1)S(1)} %copy-done.1, f32[512,4096]{1,0:T(8,128)} %reduce-scatter.6.cloned.1.call-done, bf16[512,4096]{1,0:T(8,128)(2,1)} %convolution_convert_fusion), kind=kOutput, calls=%fused_computation.7 | convolution fusion | flops 8613003264 | bytes 48234496 | tf_op jit(solution)/shard_map/dot_general | solution.py:45
  678.0 0.1 reduce-scatter.12.cloned.1.call-update
  678.1 0.3 reduce-scatter.14.cloned.1.call-start
  678.4 73.3 %all-gather.14.cloned.1.call-done = bf16[512,16384]{1,0:T(8,128)(2,1)} async-done(((bf16[512,4096]{1,0:T(8,128)(2,1)}), bf16[512,16384]{1,0:T(8,128)(2,1)}) %all-gather.14.cloned.1.call-update) | async-done | bytes 16777232 | tf_op jit(solution)/shard_map/all_gather | solution.py:37
  751.7 21.3 %fusion.13 = f32[16384,512]{1,0:T(8,128)} fusion(bf16[512,16384]{1,0:T(8,128)(2,1)} %all-gather.14.cloned.1.call-done, bf16[512,512]{1,0:T(8,128)(2,1)S(1)} %copy-done), kind=kOutput, calls=%fused_computation.28 | convolution fusion | flops 8589934592 | bytes 50855936 | tf_op jit(solution)/shard_map/dot_general | solution.py:38
  772.9 0.1 reduce-scatter.14.cloned.1.call-update
  773.0 26.3 %reduce-scatter.8.cloned.1.call-done = f32[512,512]{1,0:T(8,128)} async-done(((f32[512,2048]{1,0:T(8,128)}), f32[512,512]{1,0:T(8,128)}) %reduce-scatter.8.cloned.1.call-update) | async-done | bytes 1048592 | tf_op jit(solution)/shard_map/reduce_scatter | solution.py:43
  799.3 2.1 convert_element_type.30
  801.4 167.8 %reduce-scatter.10.cloned.1.call-done = f32[256,4096]{0,1:T(8,128)} async-done(((f32[2048,4096]{0,1:T(8,128)}), f32[256,4096]{0,1:T(8,128)}) %reduce-scatter.10.cloned.1.call-update) | async-done | bytes 4194320 | tf_op jit(solution)/shard_map/reduce_scatter | solution.py:44
  969.1 5.6 copy.9
  974.7 164.4 %reduce-scatter.12.cloned.1.call-done = f32[256,4096]{0,1:T(8,128)} async-done(((f32[2048,4096]{0,1:T(8,128)}), f32[256,4096]{0,1:T(8,128)}) %reduce-scatter.12.cloned.1.call-update) | async-done | bytes 4194320 | tf_op jit(solution)/shard_map/reduce_scatter | solution.py:45
  1139.2 5.6 copy.10
  1144.7 164.9 %reduce-scatter.14.cloned.1.call-done = f32[2048,512]{1,0:T(8,128)} async-done(((f32[16384,512]{1,0:T(8,128)}), f32[2048,512]{1,0:T(8,128)}) %reduce-scatter.14.cloned.1.call-update) | async-done | bytes 4194320 | tf_op jit(solution)/shard_map/reduce_scatter | solution.py:39
Async XLA Ops:
  7.2 89.4 %copy-start = (bf16[512,512]{1,0:T(8,128)(2,1)S(1)}, bf16[512,512]{1,0:T(8,128)(2,1)}, u32[]{:S(2)}) copy-start(bf16[512,512]{1,0:T(8,128)(2,1)} %param.6) | copy-start | bytes 1572868
  7.2 89.4 %all-gather.6.cloned.1.call-start = ((), (), s32[]{:S(2)}) async-start(), calls=%async_computation.5 | async-start | bytes 18874368 | tf_op jit(solution)/shard_map/all_gather | solution.py:29
  8.0 118.2 %all-gather.8.cloned.1.call-start = ((), (), s32[]{:S(2)}) async-start(), calls=%async_computation.7 | async-start | bytes 2621440 | tf_op jit(solution)/shard_map/all_gather | solution.py:26
  8.8 202.2 %all-gather.12.cloned.1.call-start = ((), (), s32[]{:S(2)}) async-start(), calls=%async_computation.9 | async-start | bytes 18874368 | tf_op jit(solution)/shard_map/all_gather | solution.py:27
  9.6 286.1 %all-gather.10.cloned.1.call-start = ((), (), s32[]{:S(2)}) async-start(), calls=%async_computation.8 | async-start | bytes 18874368 | tf_op jit(solution)/shard_map/all_gather | solution.py:28
  10.2 567.9 %reduce-scatter.6.cloned.1.call-start = ((), (), s32[]{:S(2)}) async-start(), calls=%async_computation.6 | async-start | bytes 41943040 | tf_op jit(solution)/shard_map/reduce_scatter | solution.py:36
  119.8 631.9 %all-gather.14.cloned.1.call-start = ((), (), s32[]{:S(2)}) async-start(), calls=%async_computation.13 | async-start | bytes 20971520 | tf_op jit(solution)/shard_map/all_gather | solution.py:37
  126.2 452.0 %copy-start.1 = (bf16[512,2048]{1,0:T(8,128)(2,1)S(1)}, bf16[512,2048]{1,0:T(8,128)(2,1)}, u32[]{:S(2)}) copy-start(bf16[512,2048]{1,0:T(8,128)(2,1)} %all-gather.8.cloned.1.call-done) | copy-start | bytes 6291460
  599.5 199.8 %reduce-scatter.8.cloned.1.call-start = ((), (), s32[]{:S(2)}) async-start(), calls=%async_computation.10 | async-start | bytes 5242880 | tf_op jit(solution)/shard_map/reduce_scatter | solution.py:43
  635.5 333.6 %reduce-scatter.10.cloned.1.call-start = ((), (), s32[]{:S(2)}) async-start(), calls=%async_computation.11 | async-start | bytes 37748736 | tf_op jit(solution)/shard_map/reduce_scatter | solution.py:44
  653.5 485.7 %reduce-scatter.12.cloned.1.call-start = ((), (), s32[]{:S(2)}) async-start(), calls=%async_computation.12 | async-start | bytes 37748736 | tf_op jit(solution)/shard_map/reduce_scatter | solution.py:45
  678.1 631.5 %reduce-scatter.14.cloned.1.call-start = ((), (), s32[]{:S(2)}) async-start(), calls=%async_computation.14 | async-start | bytes 37748736 | tf_op jit(solution)/shard_map/reduce_scatter | solution.py:39
Sparse Core Ops, SparseCore 0:
  9.6 86.9 all-gather.5
  98.2 27.9 all-gather.7
  127.8 83.1 all-gather.11
  212.5 83.1 all-gather.9
  297.9 280.1 reduce-scatter.5
  599.6 152.0 all-gather.13
  754.0 45.2 reduce-scatter.7
  801.7 167.4 reduce-scatter.9
  971.5 167.5 reduce-scatter.11
  1142.0 167.6 reduce-scatter.13
where the time goes:
time: 1320 us
  waiting for transfers between devices  1130 us (86%)
  matrix products  157 us (12%)
  between operations  14.4 us (1%)
    reduce_scatter x1, waiting for transfers between devices, block_backward(): lax.psum_scatter(grad_h_part, 'col', scatter_dimension=1, tiled=True)  282 us
    reduce_scatter x1, waiting for transfers between devices, block_backward(): lax.psum_scatter(lax.dot_general(x_band, grad_gate, COL_DIMS, preferred_e...  168 us
    reduce_scatter x1, waiting for transfers between devices, block_backward(): lax.psum_scatter(dw_out_part, 'row', scatter_dimension=0, tiled=True)  165 us
    reduce_scatter x1, waiting for transfers between devices, block_backward(): lax.psum_scatter(lax.dot_general(x_band, grad_up, COL_DIMS, preferred_ele...  164 us
    all_gather x1, waiting for transfers between devices, block_backward(): out_band = lax.all_gather(out_blk, 'row', axis=0, tiled=True)  86.3 us
    all_gather x1, waiting for transfers between devices, block_backward(): gate_band = lax.all_gather(gate_blk, 'row', axis=0, tiled=True)  84.9 us
    all_gather x1, waiting for transfers between devices, block_backward(): hidden_band = lax.all_gather(hidden, 'col', axis=1, tiled=True)  73.3 us
    all_gather x1, waiting for transfers between devices, block_backward(): up_band = lax.all_gather(up_blk, 'row', axis=0, tiled=True)  70.4 us
  transfers between devices with their start and end apart: 10, of which 10 were waited for; matrix products, arithmetic and copies ran while one was open for 11% of the time, Pallas kernels for 0%

commit v1 on v0

v1 whole, which is shorter than its diff:
```python
import math
import jax
import jax.numpy as jnp
from jax import lax
from jax.sharding import PartitionSpec as P

GELU_SCALE = math.sqrt(2.0 / math.pi)
ROW_DIMS = (((1,), (1,)), ((), ()))
COL_DIMS = (((0,), (0,)), ((), ()))


def gelu_pair(pre_act):
    pre_f32 = pre_act.astype(jnp.float32)
    inner_arg = GELU_SCALE * (pre_f32 + 0.044715 * pre_f32 * pre_f32 * pre_f32)
    tanh_val = jnp.tanh(inner_arg)
    gelu_val = 0.5 * pre_f32 * (1.0 + tanh_val)
    gelu_der = 0.5 * (1.0 + tanh_val) + 0.5 * pre_f32 * (1.0 - tanh_val * tanh_val) * GELU_SCALE * (1.0 + 3.0 * 0.044715 * pre_f32 * pre_f32)
    return gelu_val, gelu_der


def solution(mesh):
    act_spec = P(("dp", "row"), "col")
    weight_spec = P("row", "col")
    n_row, n_col = mesh.shape["row"], mesh.shape["col"]

    to_slice, from_slice = [], []
    for r in range(n_row):
        for c in range(n_col):
            k = r * n_col + c
            dst = (k // n_row) * n_row + k % n_row
            to_slice.append((c * n_row + r, dst))
            from_slice.append((dst, c * n_row + r))

    def block_backward(x_blk, gy_blk, gate_blk, up_blk, out_blk):
        gate = lax.all_to_all(gate_blk, "row", split_axis=1, concat_axis=0, tiled=True)
        up = lax.all_to_all(up_blk, "row", split_axis=1, concat_axis=0, tiled=True)
        out = lax.all_to_all(out_blk, "col", split_axis=0, concat_axis=1, tiled=True)
        out = lax.ppermute(out, ("col", "row"), to_slice)
        x_all = lax.all_gather(lax.all_gather(x_blk, "col", axis=1, tiled=True), "row", axis=0, tiled=True)
        gy_all = lax.all_gather(lax.all_gather(gy_blk, "col", axis=1, tiled=True), "row", axis=0, tiled=True)
        pre_gate = jnp.dot(x_all, gate, preferred_element_type=jnp.float32).astype(jnp.bfloat16)
        pre_up = jnp.dot(x_all, up, preferred_element_type=jnp.float32).astype(jnp.bfloat16)
        gelu_val, gelu_der = gelu_pair(pre_gate)
        up_f32 = pre_up.astype(jnp.float32)
        hidden = (gelu_val * up_f32).astype(jnp.bfloat16)
        grad_h = lax.dot_general(gy_all, out, ROW_DIMS, preferred_element_type=jnp.float32)
        grad_gate = (grad_h * up_f32 * gelu_der).astype(jnp.bfloat16)
        grad_up = (grad_h * gelu_val).astype(jnp.bfloat16)
        grad_x_part = lax.dot_general(grad_gate, gate, ROW_DIMS, preferred_element_type=jnp.float32) + lax.dot_general(grad_up, up, ROW_DIMS, preferred_element_type=jnp.float32)
        grad_x = lax.psum_scatter(grad_x_part, "row", scatter_dimension=0, tiled=True)
        grad_x = lax.psum_scatter(grad_x, "col", scatter_dimension=1, tiled=True).astype(jnp.bfloat16)
        dw_gate = lax.dot_general(x_all, grad_gate, COL_DIMS, preferred_element_type=jnp.float32)
        dw_gate = lax.all_to_all(dw_gate, "row", split_axis=0, concat_axis=1, tiled=True)
        dw_up = lax.dot_general(x_all, grad_up, COL_DIMS, preferred_element_type=jnp.float32)
        dw_up = lax.all_to_all(dw_up, "row", split_axis=0, concat_axis=1, tiled=True)
        dw_out = lax.dot_general(hidden, gy_all, COL_DIMS, preferred_element_type=jnp.float32)
        dw_out = lax.ppermute(dw_out, ("col", "row"), from_slice)
        dw_out = lax.all_to_all(dw_out, "col", split_axis=1, concat_axis=0, tiled=True)
        return grad_x, dw_gate, dw_up, dw_out

    return jax.shard_map(block_backward, mesh=mesh, in_specs=(act_spec, act_spec, weight_spec, weight_spec, weight_spec), out_specs=(act_spec, act_spec, act_spec, act_spec), check_vma=False)
```

time: 1320 us -> 942 us (0.71)
  waiting for transfers between devices: 1130 us -> 681 us
  starting transfers between devices: 1.83 us -> 42.3 us
  local copies, waits for them, and re-layouts: 11.2 us -> 42.6 us
    reduce_scatter x5 -> x2, waiting for transfers between devices: 806 us -> 348 us  [the longest x1 348 us: block_backward(): lax.psum_scatter(grad_x_part, 'row', scatter_dimension=0, tiled=True)]
    all_to_all x0 -> x6, waiting for transfers between devices: none -> 173 us  [the longest x1 44.9 us: block_backward(): lax.all_to_all(gate_blk, 'row', split_axis=1, concat_axis=0, tiled=True)]
    all_gather x5 -> x4, waiting for transfers between devices: 321 us -> 157 us  [the longest x1 94.8 us: block_backward(): lax.all_gather(lax.all_gather(gy_blk, 'col', axis=1, tiled=True), 'row',...]
    all_to_all x0 -> x6, starting transfers between devices: none -> 33.5 us  [the longest x1 8.78 us: block_backward(): lax.all_to_all(dw_up, 'row', split_axis=0, concat_axis=1, tiled=True)]
    all_to_all x0 -> x6, local copies, waits for them, and re-layouts: none -> 18.7 us  [the longest x1 4.74 us: block_backward(): lax.all_to_all(dw_out, 'col', split_axis=1, concat_axis=0, tiled=True)]
  transfers between devices with their start and end apart: 10 -> 14, of which waited for: 10 -> 10; matrix products, arithmetic and copies ran while one was open for 11% -> 11% of each run, Pallas kernels for 0% -> 0%
where the time goes in v1:
time: 942 us; the launch traced here: 931 us
  waiting for transfers between devices  681 us (72%)
  matrix products  148 us (16%)
  local copies, waits for them, and re-layouts  42.6 us (5%)
  starting transfers between devices  42.3 us (4%)
  between operations  14.7 us (2%)
    reduce_scatter x1, waiting for transfers between devices, block_backward(): lax.psum_scatter(grad_x_part, 'row', scatter_dimension=0, tiled=True)  348 us
    all_gather x1, waiting for transfers between devices, block_backward(): lax.all_gather(lax.all_gather(gy_blk, 'col', axis=1, tiled=True), 'row',...  94.8 us
    all_to_all x1, waiting for transfers between devices, block_backward(): lax.all_to_all(gate_blk, 'row', split_axis=1, concat_axis=0, tiled=True)  44.9 us
    all_to_all x1, waiting for transfers between devices, block_backward(): lax.all_to_all(dw_up, 'row', split_axis=0, concat_axis=1, tiled=True)  43.9 us
    all_to_all x1, waiting for transfers between devices, block_backward(): lax.all_to_all(dw_out, 'col', split_axis=1, concat_axis=0, tiled=True)  36.4 us
    all_gather x1, waiting for transfers between devices, block_backward(): lax.all_gather(x_blk, 'col', axis=1, tiled=True)  32.5 us
    dot_general x1, matrix products, block_backward(): lax.dot_general(grad_up, up, ROW_DIMS, preferred_element_type=jnp.float32)  31.3 us
    all_gather x1, waiting for transfers between devices, block_backward(): lax.all_gather(gy_blk, 'col', axis=1, tiled=True)  29.5 us
  transfers between devices with their start and end apart: 14, of which 10 were waited for; matrix products, arithmetic and copies ran while one was open for 11% of the time, Pallas kernels for 0%

profile of v1, /device:TPU:97, one launch (start us, length us, event | category | flops | bytes accessed | tf_op | source)
XLA Modules:
  0.0 931.0 jit_solution(6115689401131930837)
XLA Ops:
  7.2 0.1 all-gather.9.cloned.1.call-start
  7.2 0.7 all-gather.9.cloned.1.call-update
  8.0 0.1 all-gather.5.cloned.1.call-start
  8.0 0.7 all-gather.5.cloned.1.call-update
  8.8 0.1 all-gather.11.cloned.1.call-start
  8.9 32.5 %all-gather.9.cloned.1.call-done = bf16[512,2048]{1,0:T(8,128)(2,1)} async-done(((bf16[512,512]{1,0:T(8,128)(2,1)}), bf16[512,2048]{1,0:T(8,128)(2,1)}) %all-gather.9.cloned.1.call-update) | async-done | bytes 2097168 | tf_op jit(solution)/shard_map/all_gather | solution.py:39
  41.3 0.1 all-gather.11.cloned.1.call-update
  41.4 0.1 all-gather.7.cloned.1.call-start
  41.5 29.5 %all-gather.5.cloned.1.call-done = bf16[512,2048]{1,0:T(8,128)(2,1)} async-done(((bf16[512,512]{1,0:T(8,128)(2,1)}), bf16[512,2048]{1,0:T(8,128)(2,1)}) %all-gather.5.cloned.1.call-update) | async-done | bytes 2097168 | tf_op jit(solution)/shard_map/all_gather | solution.py:40
  70.9 0.1 all-gather.7.cloned.1.call-update
  71.0 3.7 all-to-all-start
  74.7 4.1 copy.26
  78.8 21.1 %all-to-all-done = bf16[4,512,512]{2,1,0:T(8,128)(2,1)S(1)} async-done(((bf16[4,512,512]{2,1,0:T(8,128)(2,1)}), bf16[4,512,512]{2,1,0:T(8,128)(2,1)S(1)}, u32[]{:S(2)}, u32[]{:S(2)}) %all-to-all-start) | async-done | bytes 2097184 | tf_op jit(solution)/shard_map/all_to_all | solution.py:37
  99.9 6.3 all-to-all-start.2
  106.2 4.1 copy.24
  110.2 44.9 %all-to-all-done.2 = bf16[256,8,512]{0,2,1:T(8,128)(2,1)} async-done(((bf16[256,8,512]{0,2,1:T(8,128)(2,1)}), bf16[256,8,512]{0,2,1:T(8,128)(2,1)}, u32[]{:S(2)}, u32[]{:S(2)}) %all-to-all-start.2) | async-done | bytes 2097184 | tf_op jit(solution)/shard_map/all_to_all | solution.py:35
  155.2 5.1 all-to-all-start.1
  160.3 0.0 reduce-scatter.3.cloned.1.call-start
  160.3 2.4 copy.23
  162.6 5.1 collective-permute-start
  167.8 4.0 copy.27
  171.7 27.0 %all-to-all-done.1 = bf16[256,8,512]{0,2,1:T(8,128)(2,1)} async-done(((bf16[256,8,512]{0,2,1:T(8,128)(2,1)}), bf16[256,8,512]{0,2,1:T(8,128)(2,1)}, u32[]{:S(2)}, u32[]{:S(2)}) %all-to-all-start.1) | async-done | bytes 2097184 | tf_op jit(solution)/shard_map/all_to_all | solution.py:36
  198.8 2.9 copy.25
  201.6 0.0 copy-start.1
  201.6 0.0 all-gather.11.cloned.1.call-done
  201.7 14.5 %convolution_convert_fusion.1 = bf16[4096,512]{1,0:T(8,128)(2,1)} fusion(bf16[4096,2048]{1,0:T(8,128)(2,1)} %all-gather.11.cloned.1.call-done, bf16[2048,512]{1,0:T(8,128)(2,1)S(1)} %bitcast.48), kind=kOutput, calls=%fused_computation.23 | convolution fusion | flops 8592031744 | bytes 23068672 | tf_op jit(solution)/shard_map/dot_general | solution.py:42
  216.1 0.0 copy-done.1
  216.2 1.9 collective-permute-done
  218.0 94.8 %all-gather.7.cloned.1.call-done = bf16[4096,2048]{1,0:T(8,128)(2,1)} async-done(((bf16[512,2048]{1,0:T(8,128)(2,1)}), bf16[4096,2048]{1,0:T(8,128)(2,1)}) %all-gather.7.cloned.1.call-update) | async-done | bytes 16777232 | tf_op jit(solution)/shard_map/all_gather | solution.py:40
  312.9 12.7 %fusion.22 = f32[4096,512]{1,0:T(8,128)S(1)} fusion(bf16[4096,2048]{1,0:T(8,128)(2,1)} %all-gather.7.cloned.1.call-done, bf16[512,2048]{0,1:T(8,128)(2,1)} %collective-permute-done), kind=kOutput, calls=%fused_computation.37 | convolution fusion | flops 8589934592 | bytes 27262976 | tf_op jit(solution)/shard_map/dot_general | solution.py:46
  325.6 0.0 copy-start
  325.6 24.2 %fusion.6 = (bf16[4096,512]{1,0:T(8,128)(2,1)}, bf16[4096,512]{1,0:T(8,128)(2,1)}) fusion(f32[4096,512]{1,0:T(8,128)S(1)} %fusion.22, bf16[4096,512]{1,0:T(8,128)(2,1)} %convolution_convert_fusion.1, bf16[4096,2048]{1,0:T(8,128)(2,1)} %all-gather.11.cloned.1.call-done, bf16[2048,512]{1,0:T(8,128)(2,1)} %bitcast.56), kind=kOutput, calls=%fused_computation.16 | convolution fusion | flops 8638169088 | bytes 39845888 | tf_op jit(solution)/shard_map/dot_general | solution.py:41
  349.8 0.0 copy-done
  349.8 0.0 copy-start.2
  349.8 18.1 %fusion.23 = f32[4096,2048]{1,0:T(8,128)} fusion(bf16[4096,512]{1,0:T(8,128)(2,1)} %get-tuple-element.8, bf16[2048,512]{1,0:T(8,128)(2,1)} %bitcast.57), kind=kOutput, calls=%fused_computation.38 | convolution fusion | flops 8589934592 | bytes 39845888 | tf_op jit(solution)/shard_map/dot_general | solution.py:49
  367.9 0.0 copy-done.2
  367.9 31.3 %convolution_add_fusion = f32[4096,2048]{1,0:T(8,128)} fusion(f32[4096,2048]{1,0:T(8,128)} %fusion.23, bf16[2048,512]{1,0:T(8,128)(2,1)S(1)} %bitcast.49, f32[4096,512]{1,0:T(8,128)} %copy-done, bf16[4096,512]{1,0:T(8,128)(2,1)} %get-tuple-element.9), kind=kOutput, calls=%fused_computation.7 | convolution fusion | flops 8621391872 | bytes 81788928 | tf_op jit(solution)/shard_map/dot_general | solution.py:49
  399.2 0.1 reduce-scatter.3.cloned.1.call-update
  399.3 12.9 %fusion.24 = f32[512,2048]{1,0:T(8,128)S(1)} fusion(bf16[4096,512]{1,0:T(8,128)(2,1)} %get-tuple-element.8, bf16[4096,2048]{1,0:T(8,128)(2,1)} %all-gather.11.cloned.1.call-done), kind=kOutput, calls=%fused_computation.39 | convolution fusion | flops 8589934592 | bytes 25165824 | tf_op jit(solution)/shard_map/dot_general | solution.py:52
  412.2 2.4 copy.41
  414.6 4.8 all-to-all-start.3
  419.4 0.0 reduce-scatter.5.cloned.1.call-start
  419.4 17.4 %fusion.11 = f32[512,2048]{1,0:T(8,128)} fusion(bf16[4096,2048]{1,0:T(8,128)(2,1)} %all-gather.7.cloned.1.call-done, bf16[4096,512]{1,0:T(8,128)(2,1)} %convolution_convert_fusion.1, bf16[4096,512]{1,0:T(8,128)(2,1)} %get-tuple-element.9), kind=kOutput, calls=%fused_computation.24 | convolution fusion | flops 8615100416 | bytes 29360128 | tf_op jit(solution)/shard_map/dot_general | solution.py:56
  436.8 3.4 collective-permute-start.1
  440.2 347.6 %reduce-scatter.3.cloned.1.call-done = f32[512,2048]{1,0:T(8,128)} async-done(((f32[4096,2048]{1,0:T(8,128)}), f32[512,2048]{1,0:T(8,128)}) %reduce-scatter.3.cloned.1.call-update) | async-done | bytes 4194320 | tf_op jit(solution)/shard_map/reduce_scatter | solution.py:50
  787.8 0.1 reduce-scatter.5.cloned.1.call-update
  787.9 16.7 %fusion.21 = f32[512,2048]{1,0:T(8,128)S(1)} fusion(bf16[4096,2048]{1,0:T(8,128)(2,1)} %all-gather.11.cloned.1.call-done, f32[4096,512]{1,0:T(8,128)} %copy-done, bf16[4096,512]{1,0:T(8,128)(2,1)} %get-tuple-element.9), kind=kOutput, calls=%fused_computation.36 | convolution fusion | flops 8613003264 | bytes 33554432 | tf_op jit(solution)/shard_map/dot_general | solution.py:54
  804.6 2.4 copy.40
  806.9 0.0 all-to-all-done.3
  806.9 8.8 all-to-all-start.4
  815.7 0.0 collective-permute-done.1
  815.7 4.7 copy.39
  820.5 43.9 %all-to-all-done.4 = f32[8,256,512]{1,2,0:T(8,128)} async-done(((f32[8,256,512]{1,2,0:T(8,128)}), f32[8,256,512]{1,2,0:T(8,128)}, u32[]{:S(2)}, u32[]{:S(2)}) %all-to-all-start.4) | async-done | bytes 4194336 | tf_op jit(solution)/shard_map/all_to_all | solution.py:55
  864.4 4.9 all-to-all-start.5
  869.3 5.6 copy.31
  874.9 5.6 copy.32
  880.5 36.4 %all-to-all-done.5 = f32[512,4,512]{2,0,1:T(8,128)} async-done(((f32[512,4,512]{2,0,1:T(8,128)}), f32[512,4,512]{2,0,1:T(8,128)}, u32[]{:S(2)}, u32[]{:S(2)}) %all-to-all-start.5) | async-done | bytes 4194336 | tf_op jit(solution)/shard_map/all_to_all | solution.py:58
  916.9 0.0 reduce-scatter.5.cloned.1.call-done
  916.9 2.1 convert_element_type.30
  919.0 4.6 copy.43
Async XLA Ops:
  7.2 34.2 %all-gather.9.cloned.1.call-start = ((), (), s32[]{:S(2)}) async-start(), calls=%async_computation.10 | async-start | bytes 2621440 | tf_op jit(solution)/shard_map/all_gather | solution.py:39
  8.0 63.0 %all-gather.5.cloned.1.call-start = ((), (), s32[]{:S(2)}) async-start(), calls=%async_computation.8 | async-start | bytes 2621440 | tf_op jit(solution)/shard_map/all_gather | solution.py:40
  8.8 192.9 %all-gather.11.cloned.1.call-start = ((), (), s32[]{:S(2)}) async-start(), calls=%async_computation.11 | async-start | bytes 18874368 | tf_op jit(solution)/shard_map/all_gather | solution.py:39
  41.4 271.5 %all-gather.7.cloned.1.call-start = ((), (), s32[]{:S(2)}) async-start(), calls=%async_computation.9 | async-start | bytes 18874368 | tf_op jit(solution)/shard_map/all_gather | solution.py:40
  71.0 28.9 %all-to-all-start = ((bf16[4,512,512]{2,1,0:T(8,128)(2,1)}), bf16[4,512,512]{2,1,0:T(8,128)(2,1)S(1)}, u32[]{:S(2)}, u32[]{:S(2)}) async-start(bf16[4,512,512]{2,1,0:T(8,128)(2,1)} %bitcast.55), calls=%async_computation | async-start | bytes 4194304 | tf_op jit(solution)/shard_map/all_to_all | solution.py:37
  99.9 55.3 %all-to-all-start.2 = ((bf16[256,8,512]{0,2,1:T(8,128)(2,1)}), bf16[256,8,512]{0,2,1:T(8,128)(2,1)}, u32[]{:S(2)}, u32[]{:S(2)}) async-start(bf16[256,8,512]{0,2,1:T(8,128)(2,1)} %bitcast.52), calls=%async_computation.2 | async-start | bytes 4194304 | tf_op jit(solution)/shard_map/all_to_all | solution.py:35
  155.2 43.6 %all-to-all-start.1 = ((bf16[256,8,512]{0,2,1:T(8,128)(2,1)}), bf16[256,8,512]{0,2,1:T(8,128)(2,1)}, u32[]{:S(2)}, u32[]{:S(2)}) async-start(bf16[256,8,512]{0,2,1:T(8,128)(2,1)} %bitcast.51), calls=%async_computation.1 | async-start | bytes 4194304 | tf_op jit(solution)/shard_map/all_to_all | solution.py:36
  160.3 627.5 %reduce-scatter.3.cloned.1.call-start = ((), (), s32[]{:S(2)}) async-start(), calls=%async_computation.12 | async-start | bytes 37748736 | tf_op jit(solution)/shard_map/reduce_scatter | solution.py:50
  162.6 55.4 %collective-permute-start = (bf16[512,2048]{0,1:T(8,128)(2,1)}, bf16[512,2048]{0,1:T(8,128)(2,1)}, u32[]{:S(2)}, u32[]{:S(2)}) collective-permute-start(bf16[512,2048]{0,1:T(8,128)(2,1)} %bitcast.58), channel_id=1, source_target_pairs={{0,0},{8,1},{16,2},{24,3},{1,4},{9,5},{17,6},{25,7},{2,8},{10,9},{... | collective-permute-start | bytes 6291464 | tf_op jit(solution)/shard_map/ppermute | solution.py:38
  201.6 14.5 %copy-start.1 = (bf16[8,256,512]{2,1,0:T(8,128)(2,1)}, bf16[8,256,512]{2,1,0:T(8,128)(2,1)S(1)}, u32[]{:S(2)}) copy-start(bf16[8,256,512]{2,1,0:T(8,128)(2,1)S(1)} %copy.25) | copy-start | bytes 6291460
  325.6 24.2 %copy-start = (f32[4096,512]{1,0:T(8,128)}, f32[4096,512]{1,0:T(8,128)S(1)}, u32[]{:S(2)}) copy-start(f32[4096,512]{1,0:T(8,128)S(1)} %fusion.22) | copy-start | bytes 25165828
  349.8 18.1 %copy-start.2 = (bf16[8,256,512]{2,1,0:T(8,128)(2,1)S(1)}, bf16[8,256,512]{2,1,0:T(8,128)(2,1)}, u32[]{:S(2)}) copy-start(bf16[8,256,512]{2,1,0:T(8,128)(2,1)} %copy-done.1) | copy-start | bytes 6291460
  414.6 392.4 %all-to-all-start.3 = ((f32[8,256,512]{1,2,0:T(8,128)}), f32[8,256,512]{1,2,0:T(8,128)}, u32[]{:S(2)}, u32[]{:S(2)}) async-start(f32[8,256,512]{1,2,0:T(8,128)} %bitcast.45), calls=%async_computation.5 | async-start | bytes 8388608 | tf_op jit(solution)/shard_map/all_to_all | solution.py:53
  419.4 497.6 %reduce-scatter.5.cloned.1.call-start = ((), (), s32[]{:S(2)}) async-start(), calls=%async_computation.13 | async-start | bytes 5242880 | tf_op jit(solution)/shard_map/reduce_scatter | solution.py:51
  436.8 379.0 %collective-permute-start.1 = (f32[512,2048]{1,0:T(8,128)}, f32[512,2048]{1,0:T(8,128)}, u32[]{:S(2)}, u32[]{:S(2)}) collective-permute-start(f32[512,2048]{1,0:T(8,128)} %fusion.11), channel_id=1, source_target_pairs={{0,0},{1,8},{2,16},{3,24},{4,1},{5,9},{6,17},{7,25},{8,2},{9,10},{... | collective-permute-start | bytes 12582920 | tf_op jit(solution)/shard_map/ppermute | solution.py:57
  806.9 57.5 %all-to-all-start.4 = ((f32[8,256,512]{1,2,0:T(8,128)}), f32[8,256,512]{1,2,0:T(8,128)}, u32[]{:S(2)}, u32[]{:S(2)}) async-start(f32[8,256,512]{1,2,0:T(8,128)} %bitcast.46), calls=%async_computation.6 | async-start | bytes 8388608 | tf_op jit(solution)/shard_map/all_to_all | solution.py:55
  864.4 52.5 %all-to-all-start.5 = ((f32[512,4,512]{2,0,1:T(8,128)}), f32[512,4,512]{2,0,1:T(8,128)}, u32[]{:S(2)}, u32[]{:S(2)}) async-start(f32[512,4,512]{2,0,1:T(8,128)} %bitcast.47), calls=%async_computation.7 | async-start | bytes 8388608 | tf_op jit(solution)/shard_map/all_to_all | solution.py:58
Sparse Core Ops, SparseCore 0:
  9.6 31.7 all-gather.8
  42.9 27.9 all-gather.4
  72.6 128.4 all-gather.10
  202.5 110.2 all-gather.6
  399.4 388.3 reduce-scatter.2
  790.0 46.8 reduce-scatter.4

commit v2 on v1

v2 whole, which is shorter than its diff:
```python
import functools
import math
import jax
import jax.numpy as jnp
from jax import lax
from jax.experimental import pallas as pl
from jax.experimental.pallas import tpu as pltpu
from jax.sharding import PartitionSpec as P

GELU_SCALE = math.sqrt(2.0 / math.pi)
ROW_DIMS = (((1,), (1,)), ((), ()))
COL_DIMS = (((0,), (0,)), ((), ()))
MESH = pl.DeviceIdType.MESH
ANY = pl.BlockSpec(memory_space=pl.ANY)
VMEM = pl.BlockSpec(memory_space=pltpu.VMEM)
VMEM_LIMIT = 64 * 1024 * 1024 - 65536


def gelu_pair(pre_act):
    pre_f32 = pre_act.astype(jnp.float32)
    inner_arg = GELU_SCALE * (pre_f32 + 0.044715 * pre_f32 * pre_f32 * pre_f32)
    tanh_val = jnp.tanh(inner_arg)
    gelu_val = 0.5 * pre_f32 * (1.0 + tanh_val)
    gelu_der = 0.5 * (1.0 + tanh_val) + 0.5 * pre_f32 * (1.0 - tanh_val * tanh_val) * GELU_SCALE * (1.0 + 3.0 * 0.044715 * pre_f32 * pre_f32)
    return gelu_val, gelu_der


class Place:
    def __init__(self):
        row, self.y = lax.axis_index("row"), lax.axis_index("col")
        self.row = row
        self.x, self.c = lax.div(row, 2), lax.rem(row, 2)
        self.other = 1 - self.c

    def xs(self, d):
        return lax.rem(self.x + (d % 4), 4)

    def ys(self, d):
        return lax.rem(self.y + (d % 4), 4)

    def to_x(self, d, core):
        return {"row": 2 * self.xs(d) + core, "col": self.y}

    def to_y(self, d):
        return {"row": self.row, "col": self.ys(d)}

    def partner(self):
        return {"row": 2 * self.x + self.other, "col": self.y}

    def barrier(self):
        sem = pltpu.get_barrier_semaphore()
        peers = [self.to_x(d, k) for d in (1, -1) for k in (0, 1)]
        peers += [self.to_y(1), self.to_y(-1), self.partner()]
        for peer in peers:
            pl.semaphore_signal(sem, inc=1, device_id=peer, device_id_type=MESH)
        pl.semaphore_wait(sem, len(peers))


class Net:
    def __init__(self, send_sem, recv_sem):
        self.send_sem, self.recv_sem = send_sem, recv_sem
        self.ids, self.sent = {}, []

    def copy(self, tag, src, dst, peer):
        i = self.ids.setdefault(tag, len(self.ids))
        return pltpu.make_async_remote_copy(
            src_ref=src, dst_ref=dst, send_sem=self.send_sem.at[i], recv_sem=self.recv_sem.at[i],
            device_id=peer, device_id_type=MESH)

    def send(self, tag, src, dst, peer):
        copy = self.copy(tag, src, dst, peer)
        copy.start()
        self.sent.append(copy)

    def arrived(self, tag, dst, peer):
        self.copy(tag, dst, dst, peer).wait_recv()

    def finish(self):
        for copy in self.sent:
            copy.wait_send()


def rows(ref, start, size):
    return ref.at[pl.ds(pl.multiple_of(start, size), size), :]


def cols(ref, start, size):
    return ref.at[:, pl.ds(pl.multiple_of(start, size), size)]


def block(ref, row, nr, col, nc):
    return ref.at[pl.ds(pl.multiple_of(row, nr), nr), pl.ds(pl.multiple_of(col, nc), nc)]


def gather_kernel(x_ref, gy_ref, wg_ref, wu_ref, wo_ref,
                  xg, yg, wgs, wus, wos, relay_w, mid, relay_o, relay_q,
                  bounce_w, bounce_o, bounce_q, send_sem, recv_sem, local_sem):
    at = Place()
    net = Net(send_sem, recv_sem)
    tb, db = x_ref.shape
    rb = wg_ref.shape[0]
    fs = wgs.shape[1]
    gath, own = (xg, yg), (x_ref, gy_ref)
    ws, wsrc = (wgs, wus), (wg_ref, wu_ref)
    here = at.partner()

    def blk(u, dx, dy, part=None):
        row, n = (2 * at.xs(dx) + at.c) * tb, tb
        if part is not None:
            row, n = row + part * (tb // 2), tb // 2
        return block(gath[u], row, n, at.ys(dy) * db, db)

    loads = []
    for w in (0, 1):
        loads.append(pltpu.make_async_copy(cols(wsrc[w], (4 * at.c + at.x) * fs, fs), bounce_w.at[w], local_sem.at[w]))
    loads.append(pltpu.make_async_copy(rows(wo_ref, at.x * fs, fs), bounce_o, local_sem.at[2]))
    for cp in loads:
        cp.start()
    at.barrier()

    def x_piece(xd, core):
        return (4 * core + at.xs(xd)) * fs

    for u in (0, 1):
        for d in (1, -1):
            net.send(("x", u, d), own[u], blk(u, 0, 0), at.to_x(d, at.c))
            net.send(("y", u, 0, d), own[u], blk(u, 0, 0), at.to_y(d))
    stores = []
    for u in (0, 1):
        stores.append(pltpu.make_async_copy(own[u], blk(u, 0, 0), local_sem.at[3 + u]))
        stores[-1].start()
    for d in (1, -1):
        net.send(("o", d), rows(wo_ref, at.xs(d) * fs, fs), mid.at[at.x], at.to_x(d, at.c))
        half = 0 if d == 1 else 1
        net.send(("or", d), rows(wo_ref, at.xs(2) * fs + half * (fs // 2), fs // 2), relay_o.at[half], at.to_x(d, at.c))
    for cp in loads:
        cp.wait()
    stores.append(pltpu.make_async_copy(bounce_o, mid.at[at.x], local_sem.at[2]))
    stores[-1].start()
    for w in (0, 1):
        stores.append(pltpu.make_async_copy(bounce_w.at[w], rows(ws[w], at.row * rb, rb), local_sem.at[w]))
        stores[-1].start()
    for w in (0, 1):
        mine = rows(ws[w], at.row * rb, rb)
        net.send(("wp", w), cols(wsrc[w], x_piece(0, at.other), fs), mine, at.partner())
        for d in (1, -1):
            half = 0 if d == 1 else 1
            far_core = at.c if d == 1 else at.other
            net.send(("wr", w, d), cols(wsrc[w], x_piece(2, far_core), fs), relay_w.at[w, half], at.to_x(d, at.c))
            for rel, core in ((0, at.c), (1, at.other)):
                net.send(("w", w, d, rel), cols(wsrc[w], x_piece(d, core), fs), mine, at.to_x(d, core))

    def forward_y(u, j, dx):
        for d in (1, -1):
            net.send(("y", u, j, d), blk(u, dx, 0), blk(u, dx, 0), at.to_y(d))

    def halves_y(u, j, dx):
        for d in (1, -1):
            half = 0 if d == 1 else 1
            net.arrived(("y", u, j, d), blk(u, dx, -d), here)
            net.send(("yh", u, j, d), blk(u, dx, -d, half), blk(u, dx, -d, half), at.to_y(d))

    def row_done(u, j, dx):
        for d in (1, -1):
            half = 0 if d == 1 else 1
            net.arrived(("yh", u, j, d), blk(u, dx, -2 * d, half), here)
        src = rows(gath[u], (2 * at.xs(dx) + at.c) * tb, tb)
        net.send(("p", u, j), src, src, at.partner())

    for u in (0, 1):
        for j, d in ((1, 1), (2, -1)):
            half = 0 if d == 1 else 1
            net.arrived(("x", u, d), blk(u, -d, 0), here)
            net.send(("xh", u, d), blk(u, -d, 0, half), blk(u, -d, 0, half), at.to_x(d, at.c))
            forward_y(u, j, -d)
    for cp in stores:
        cp.wait()
    for d in (1, -1):
        half = 0 if d == 1 else 1
        net.arrived(("or", d), relay_o.at[half], here)
        net.send(("of", d), relay_o.at[half], mid.at[at.xs(-d), pl.ds(half * (fs // 2), fs // 2), :], at.to_x(d, at.c))
    for u in (0, 1):
        halves_y(u, 0, 0)
    for d in (1, -1):
        half = 0 if d == 1 else 1
        net.arrived(("o", d), mid.at[at.xs(-d)], here)
        net.arrived(("of", d), mid.at[at.xs(-2 * d), pl.ds(half * (fs // 2), fs // 2), :], here)
    load = pltpu.make_async_copy(mid.at[at.y], bounce_q, local_sem.at[2])
    load.start()
    for d in (1, -1):
        half = 0 if d == 1 else 1
        net.send(("q", d), mid.at[at.ys(d)], cols(wos, at.y * db, db), at.to_y(d))
        net.send(("qr", d), mid.at[at.ys(2), pl.ds(half * (fs // 2), fs // 2), :], relay_q.at[half], at.to_y(d))
    load.wait()
    store = pltpu.make_async_copy(bounce_q, cols(wos, at.y * db, db), local_sem.at[2])
    store.start()
    for u in (0, 1):
        for d in (1, -1):
            half = 0 if d == 1 else 1
            net.arrived(("xh", u, d), blk(u, -2 * d, 0, half), here)
        forward_y(u, 3, 2)
    for w in (0, 1):
        for d in (1, -1):
            half = 0 if d == 1 else 1
            core = at.c if d == 1 else at.other
            net.arrived(("wr", w, d), relay_w.at[w, half], here)
            net.send(("wf", w, d), relay_w.at[w, half], rows(ws[w], (2 * at.xs(-d) + at.c) * rb, rb), at.to_x(d, core))
    for u in (0, 1):
        row_done(u, 0, 0)
    for d in (1, -1):
        half = 0 if d == 1 else 1
        net.arrived(("qr", d), relay_q.at[half], here)
        net.send(("qf", d), relay_q.at[half], block(wos, half * (fs // 2), fs // 2, at.ys(-d) * db, db), at.to_y(d))
    for j, dx in ((1, -1), (2, 1), (3, 2)):
        for u in (0, 1):
            halves_y(u, j, dx)
        for u in (0, 1):
            row_done(u, j, dx)
    for d in (1, -1):
        half = 0 if d == 1 else 1
        net.arrived(("q", d), cols(wos, at.ys(-d) * db, db), here)
        net.arrived(("qf", d), block(wos, half * (fs // 2), fs // 2, at.ys(-2 * d) * db, db), here)
    for w in (0, 1):
        net.arrived(("wp", w), rows(ws[w], (2 * at.x + at.other) * rb, rb), here)
        for d in (1, -1):
            for rel, core in ((0, at.c), (1, at.other)):
                net.arrived(("w", w, d, rel), rows(ws[w], (2 * at.xs(-d) + core) * rb, rb), here)
            core = at.c if d == 1 else at.other
            net.arrived(("wf", w, d), rows(ws[w], (2 * at.xs(-2 * d) + core) * rb, rb), here)
    for j, dx in ((0, 0), (1, -1), (2, 1), (3, 2)):
        for u in (0, 1):
            net.arrived(("p", u, j), rows(gath[u], (2 * at.xs(dx) + at.other) * tb, tb), here)
    store.wait()
    net.finish()


def scatter_kernel(dxp, dg, du, do, dx_out, dg_out, du_out, do_out, relay_w, mid, relay_q, relay_o,
                   part, own, yh, yf, xh, xf, bounce_w, bounce_o, send_sem, recv_sem, local_sem):
    at = Place()
    net = Net(send_sem, recv_sem)
    tb, db = dx_out.shape
    rb = dg_out.shape[0]
    fs = dg.shape[1]
    hb = tb // 2
    wsrc, ws = (dg, du), (dg_out, du_out)
    here = at.partner()
    order = (2, 1, -1, 0)

    def own_rows(dx, core):
        return rows(dxp, (2 * at.xs(dx) + core) * tb, tb)

    loads = []
    for w in (0, 1):
        loads.append(pltpu.make_async_copy(rows(wsrc[w], at.row * rb, rb), bounce_w.at[w], local_sem.at[w]))
    loads.append(pltpu.make_async_copy(cols(do, at.y * db, db), bounce_o.at[0], local_sem.at[2]))
    for cp in loads:
        cp.start()
    own_loads = [pltpu.make_async_copy(own_rows(dx, at.c), own.at[j % 2], local_sem.at[4 + j % 2]) for j, dx in enumerate(order)]
    own_loads[0].start()
    own_loads[1].start()
    at.barrier()
    for j, dx in enumerate(order):
        net.send(("p", j), own_rows(dx, at.other), part.at[j], at.partner())
    for d in (1, -1):
        half = 0 if d == 1 else 1
        net.send(("qr", d), block(do, half * (fs // 2), fs // 2, at.ys(2) * db, db), relay_q.at[half], at.to_y(d))
        net.send(("q", d), cols(do, at.ys(d) * db, db), mid.at[at.y], at.to_y(d))
    for w in (0, 1):
        mine = cols(ws[w], (4 * at.c + at.x) * fs, fs)

        def piece(xd, core):
            return rows(wsrc[w], (2 * at.xs(xd) + core) * rb, rb)

        for d in (1, -1):
            half = 0 if d == 1 else 1
            far_core = at.c if d == 1 else at.other
            net.send(("wr", w, d), piece(2, far_core), relay_w.at[w, half], at.to_x(d, at.c))
        for d in (1, -1):
            for rel, core in ((0, at.c), (1, at.other)):
                net.send(("w", w, d, rel), piece(d, core), mine, at.to_x(d, core))
        net.send(("wp", w), piece(0, at.other), mine, at.partner())
    for cp in loads:
        cp.wait()
    stores = [pltpu.make_async_copy(bounce_w.at[w], cols(ws[w], (4 * at.c + at.x) * fs, fs), local_sem.at[w]) for w in (0, 1)]
    stores.append(pltpu.make_async_copy(bounce_o.at[0], mid.at[at.y], local_sem.at[2]))
    for cp in stores:
        cp.start()

    def y_cols(d):
        return pl.ds(pl.multiple_of(at.ys(d) * db, db), db)

    for j, dx in enumerate(order):
        net.arrived(("p", j), part.at[j], here)
        own_loads[j].wait()
        part[j] = part[j] + own[j % 2]
        if j + 2 < 4:
            own_loads[j + 2].start()
        for d in (1, -1):
            half = 0 if d == 1 else 1
            net.send(("yh", j, d), part.at[j, pl.ds(half * hb, hb), y_cols(2)], yh.at[j, half], at.to_y(d))
    for cp in stores:
        cp.wait()
    for d in (1, -1):
        half = 0 if d == 1 else 1
        net.arrived(("qr", d), relay_q.at[half], here)
        net.send(("qf", d), relay_q.at[half], mid.at[at.ys(-d), pl.ds(half * (fs // 2), fs // 2), :], at.to_y(d))
    for w in (0, 1):
        for d in (1, -1):
            half = 0 if d == 1 else 1
            core = at.c if d == 1 else at.other
            net.arrived(("wr", w, d), relay_w.at[w, half], here)
            src_piece = (4 * at.c + at.xs(-d)) * fs
            net.send(("wf", w, d), relay_w.at[w, half], cols(ws[w], src_piece, fs), at.to_x(d, core))
    for j, dx in enumerate(order):
        for d in (1, -1):
            half = 0 if d == 1 else 1
            net.arrived(("yh", j, d), yh.at[j, half], here)
            here_rows = pl.ds(half * hb, hb)
            part[j, here_rows, y_cols(d)] = part[j, here_rows, y_cols(d)] + yh[j, half]
            net.send(("yf", j, d), part.at[j, :, y_cols(d)], yf.at[j, half], at.to_y(d))
    for d in (1, -1):
        half = 0 if d == 1 else 1
        net.arrived(("q", d), mid.at[at.ys(-d)], here)
        net.arrived(("qf", d), mid.at[at.ys(-2 * d), pl.ds(half * (fs // 2), fs // 2), :], here)
    load = pltpu.make_async_copy(mid.at[at.x], bounce_o.at[1], local_sem.at[2])
    load.start()
    for d in (1, -1):
        half = 0 if d == 1 else 1
        net.send(("or", d), mid.at[at.xs(2), pl.ds(half * (fs // 2), fs // 2), :], relay_o.at[half], at.to_x(d, at.c))
    for d in (1, -1):
        net.send(("o", d), mid.at[at.xs(d)], rows(do_out, at.x * fs, fs), at.to_x(d, at.c))
    load.wait()
    store = pltpu.make_async_copy(bounce_o.at[1], rows(do_out, at.x * fs, fs), local_sem.at[2])
    store.start()
    for j, dx in enumerate(order):
        for d in (1, -1):
            half = 0 if d == 1 else 1
            net.arrived(("yf", j, d), yf.at[j, half], here)
        yf[j, 0] = yf[j, 0] + yf[j, 1] + part[j, :, y_cols(0)]
        if j == 0:
            for d in (1, -1):
                half = 0 if d == 1 else 1
                net.send(("xh", d), yf.at[0, 0, pl.ds(half * hb, hb), :], xh.at[half], at.to_x(d, at.c))
    for d in (1, -1):
        half = 0 if d == 1 else 1
        net.arrived(("or", d), relay_o.at[half], here)
        net.send(("of", d), relay_o.at[half], block(do_out, at.xs(-d) * fs + half * (fs // 2), fs // 2, 0, db), at.to_x(d, at.c))
    for d in (1, -1):
        half, j = (0, 1) if d == 1 else (1, 2)
        net.arrived(("xh", d), xh.at[half], here)
        here_rows = pl.ds(half * hb, hb)
        yf[j, 0, here_rows, :] = yf[j, 0, here_rows, :] + xh[half]
        net.send(("xf", d), yf.at[j, 0], xf.at[half], at.to_x(d, at.c))
    for d in (1, -1):
        half = 0 if d == 1 else 1
        net.arrived(("xf", d), xf.at[half], here)
    dx_out[...] = (yf[3, 0] + xf[0] + xf[1]).astype(dx_out.dtype)
    for d in (1, -1):
        half = 0 if d == 1 else 1
        net.arrived(("o", d), rows(do_out, at.xs(-d) * fs, fs), here)
        net.arrived(("of", d), block(do_out, at.xs(-2 * d) * fs + half * (fs // 2), fs // 2, 0, db), here)
    for w in (0, 1):
        net.arrived(("wp", w), cols(ws[w], (4 * at.other + at.x) * fs, fs), here)
        for d in (1, -1):
            for rel, core in ((0, at.c), (1, at.other)):
                net.arrived(("w", w, d, rel), cols(ws[w], (4 * core + at.xs(-d)) * fs, fs), here)
            core = at.c if d == 1 else at.other
            net.arrived(("wf", w, d), cols(ws[w], (4 * core + at.xs(-2 * d)) * fs, fs), here)
    store.wait()
    net.finish()


def gather(x_blk, gy_blk, gate_blk, up_blk, out_blk):
    (tb, db), (rb, fcol) = x_blk.shape, gate_blk.shape
    t, d, fs = 8 * tb, 4 * db, fcol // 8
    bf = jnp.bfloat16
    outs = [(t, d), (t, d), (d, fs), (d, fs), (fs, d),
            (2, 2, rb, fs), (4, fs, db), (2, fs // 2, db), (2, fs // 2, db)]
    got = pl.pallas_call(
        gather_kernel,
        name="gather_inputs",
        out_shape=[jax.ShapeDtypeStruct(s, bf) for s in outs],
        in_specs=[VMEM, VMEM, ANY, ANY, ANY],
        out_specs=[ANY] * len(outs),
        scratch_shapes=[
            pltpu.VMEM((2, rb, fs), bf), pltpu.VMEM((fs, db), bf), pltpu.VMEM((fs, db), bf),
            pltpu.SemaphoreType.DMA((80,)), pltpu.SemaphoreType.DMA((80,)), pltpu.SemaphoreType.DMA((5,)),
        ],
        compiler_params=pltpu.CompilerParams(collective_id=0, has_side_effects=True),
    )(x_blk, gy_blk, gate_blk, up_blk, out_blk)
    return got[:5]


def scatter(dxp, dg, du, do, like_x, like_w):
    (tb, db), (rb, fcol) = like_x.shape, like_w.shape
    fs = fcol // 8
    f32 = jnp.float32
    outs = [((tb, db), jnp.bfloat16), ((rb, fcol), f32), ((rb, fcol), f32), ((4 * fs, db), f32),
            ((2, 2, rb, fs), f32), ((4, fs, db), f32), ((2, fs // 2, db), f32), ((2, fs // 2, db), f32)]
    got = pl.pallas_call(
        scatter_kernel,
        name="scatter_results",
        out_shape=[jax.ShapeDtypeStruct(*s) for s in outs],
        in_specs=[ANY] * 4,
        out_specs=[VMEM] + [ANY] * (len(outs) - 1),
        scratch_shapes=[
            pltpu.VMEM((4, tb, 4 * db), f32), pltpu.VMEM((2, tb, 4 * db), f32),
            pltpu.VMEM((4, 2, tb // 2, db), f32), pltpu.VMEM((4, 2, tb, db), f32),
            pltpu.VMEM((2, tb // 2, db), f32), pltpu.VMEM((2, tb, db), f32),
            pltpu.VMEM((2, rb, fs), f32), pltpu.VMEM((2, fs, db), f32),
            pltpu.SemaphoreType.DMA((64,)), pltpu.SemaphoreType.DMA((64,)), pltpu.SemaphoreType.DMA((6,)),
        ],
        compiler_params=pltpu.CompilerParams(collective_id=1, has_side_effects=True, vmem_limit_bytes=VMEM_LIMIT),
    )(dxp, dg, du, do)
    return got[:4]


def solution(mesh):
    act_spec = P(("dp", "row"), "col")
    weight_spec = P("row", "col")
    assert mesh.shape["row"] == 8 and mesh.shape["col"] == 4

    def block_backward(x_blk, gy_blk, gate_blk, up_blk, out_blk):
        x_all, gy_all, gate, up, out = gather(x_blk, gy_blk, gate_blk, up_blk, out_blk)
        pre_gate = jnp.dot(x_all, gate, preferred_element_type=jnp.float32).astype(jnp.bfloat16)
        pre_up = jnp.dot(x_all, up, preferred_element_type=jnp.float32).astype(jnp.bfloat16)
        gelu_val, gelu_der = gelu_pair(pre_gate)
        up_f32 = pre_up.astype(jnp.float32)
        hidden = (gelu_val * up_f32).astype(jnp.bfloat16)
        grad_h = lax.dot_general(gy_all, out, ROW_DIMS, preferred_element_type=jnp.float32)
        grad_gate = (grad_h * up_f32 * gelu_der).astype(jnp.bfloat16)
        grad_up = (grad_h * gelu_val).astype(jnp.bfloat16)
        grad_x_part = lax.dot_general(grad_gate, gate, ROW_DIMS, preferred_element_type=jnp.float32) + lax.dot_general(grad_up, up, ROW_DIMS, preferred_element_type=jnp.float32)
        dw_gate = lax.dot_general(x_all, grad_gate, COL_DIMS, preferred_element_type=jnp.float32)
        dw_up = lax.dot_general(x_all, grad_up, COL_DIMS, preferred_element_type=jnp.float32)
        dw_out = lax.dot_general(hidden, gy_all, COL_DIMS, preferred_element_type=jnp.float32)
        return tuple(scatter(grad_x_part, dw_gate, dw_up, dw_out, x_blk, gate_blk))

    return jax.shard_map(block_backward, mesh=mesh, in_specs=(act_spec, act_spec, weight_spec, weight_spec, weight_spec), out_specs=(act_spec, act_spec, act_spec, act_spec), check_vma=False)
```

time: 942 us -> 576 us (0.61)
  waiting for transfers between devices: 681 us -> 0 us
  Pallas kernels: 0 us -> 411 us
  starting transfers between devices: 42.3 us -> 0 us
  local copies, waits for them, and re-layouts: 42.6 us -> 10.9 us
  between operations: 14.7 us -> 1.2 us
    pallas_call x0 -> x2, Pallas kernels: none -> 411 us  [the longest x1 222 us: scatter(): pl.pallas_call(scatter_kernel, name='scatter_results', out_shape=[jax.Sha...]
    reduce_scatter x2 -> x0, waiting for transfers between devices: 348 us -> none  [the longest x1 348 us: block_backward(): lax.psum_scatter(grad_x_part, 'row', scatter_dimension=0, tiled=True)]
    all_to_all x6 -> x0, waiting for transfers between devices: 173 us -> none  [the longest x1 44.9 us: block_backward(): lax.all_to_all(gate_blk, 'row', split_axis=1, concat_axis=0, tiled=True)]
    all_gather x4 -> x0, waiting for transfers between devices: 157 us -> none  [the longest x1 94.8 us: block_backward(): lax.all_gather(lax.all_gather(gy_blk, 'col', axis=1, tiled=True), 'row',...]
    all_to_all x6 -> x0, starting transfers between devices: 33.5 us -> none  [the longest x1 8.78 us: block_backward(): lax.all_to_all(dw_up, 'row', split_axis=0, concat_axis=1, tiled=True)]
    all_to_all x6 -> x0, local copies, waits for them, and re-layouts: 18.7 us -> none  [the longest x1 4.74 us: block_backward(): lax.all_to_all(dw_out, 'col', split_axis=1, concat_axis=0, tiled=True)]
    unnamed x11 -> x20, local copies, waits for them, and re-layouts: 24 us -> 10.9 us
  transfers between devices with their start and end apart: 14 -> 0, of which waited for: 10 -> 0; matrix products, arithmetic and copies ran while one was open for 11% -> 0% of each run, Pallas kernels for 0% -> 0%
where the time goes in v2:
time: 576 us; the launch traced here: 570 us
  Pallas kernels  411 us (71%)
  matrix products  147 us (26%)
  local copies, waits for them, and re-layouts  10.9 us (2%)
    pallas_call x1, Pallas kernels, scatter(): pl.pallas_call(scatter_kernel, name='scatter_results', out_shape=[jax.Sha...  222 us
    pallas_call x1, Pallas kernels, gather(): pl.pallas_call(gather_kernel, name='gather_inputs', out_shape=[jax.ShapeD...  189 us
    dot_general x1, matrix products, block_backward(): lax.dot_general(grad_up, up, ROW_DIMS, preferred_element_type=jnp.float32)  31.3 us
    dot_general x1, matrix products, block_backward(): jnp.dot(x_all, gate, preferred_element_type=jnp.float32)  24.2 us
    dot_general x1, matrix products, block_backward(): lax.dot_general(grad_gate, gate, ROW_DIMS, preferred_element_type=jnp.flo...  18 us
    dot_general x1, matrix products, block_backward(): lax.dot_general(hidden, gy_all, COL_DIMS, preferred_element_type=jnp.floa...  17.5 us
    dot_general x1, matrix products, block_backward(): lax.dot_general(x_all, grad_up, COL_DIMS, preferred_element_type=jnp.floa...  14.7 us
    dot_general x1, matrix products, block_backward(): jnp.dot(x_all, up, preferred_element_type=jnp.float32).astype(jnp.bfloat16)  14.5 us

profile of v2, /device:TPU:97, one launch (start us, length us, event | category | flops | bytes accessed | tf_op | source)
XLA Modules:
  0.0 569.9 jit_solution(4315113932951689639)
XLA Ops:
  0.6 189.2 %gather_inputs.1 = (bf16[4096,2048]{1,0:T(8,128)(2,1)}, bf16[4096,2048]{1,0:T(8,128)(2,1)}, bf16[2048,512]{1,0:T(8,128)(2,1)}, bf16[2048,512]{1,0:T(8,128)(2,1)}...) custom-call(bf16[512,512]{1,0:T(8,128)(2,1)} %x_ref.1, ...), custom_call_target="tpu_custom_call" | custom-call | tf_op jit(solution)/shard_map/gather_inputs/pallas_call | solution.py:379
  189.8 0.0 copy-start.6
  189.8 14.5 %convolution_convert_fusion.1 = bf16[4096,512]{1,0:T(8,128)(2,1)} fusion(bf16[4096,2048]{1,0:T(8,128)(2,1)} %get-tuple-element.15, bf16[2048,512]{1,0:T(8,128)(2,1)} %get-tuple-element.16), kind=kOutput, calls=%fused_computation.23 | convolution fusion | flops 8592031744 | bytes 23068672 | tf_op jit(solution)/shard_map/dot_general | solution.py:426
  204.3 0.0 copy-done.6
  204.3 12.5 %fusion.22 = f32[4096,512]{1,0:T(8,128)S(1)} fusion(bf16[4096,2048]{1,0:T(8,128)(2,1)} %get-tuple-element.13, bf16[512,2048]{1,0:T(8,128)(2,1)S(1)} %copy-done.6), kind=kOutput, calls=%fused_computation.34 | convolution fusion | flops 8589934592 | bytes 27262976 | tf_op jit(solution)/shard_map/dot_general | solution.py:430
  216.8 0.0 copy-start
  216.8 24.2 %fusion.6 = (bf16[4096,512]{1,0:T(8,128)(2,1)}, bf16[4096,512]{1,0:T(8,128)(2,1)}) fusion(f32[4096,512]{1,0:T(8,128)S(1)} %fusion.22, bf16[4096,512]{1,0:T(8,128)(2,1)} %convolution_convert_fusion.1, bf16[4096,2048]{1,0:T(8,128)(2,1)} %get-tuple-element.15, bf16[2048,512]{1,0:T(8,128)(2,1)} %get-tuple-element.17), kind=kOutput, calls=%fused_computation.16 | convolution fusion | flops 8638169088 | bytes 39845888 | tf_op jit(solution)/shard_map/dot_general | solution.py:425
  241.0 0.0 copy-start.7
  241.0 17.5 %fusion.11.do = f32[512,2048]{1,0:T(8,128)} fusion(bf16[4096,2048]{1,0:T(8,128)(2,1)} %get-tuple-element.13, bf16[4096,512]{1,0:T(8,128)(2,1)} %convolution_convert_fusion.1, bf16[4096,512]{1,0:T(8,128)(2,1)} %get-tuple-element.23), kind=kOutput, calls=%fused_computation.24 | convolution fusion | flops 8615100416 | bytes 29360128 | tf_op jit(solution)/shard_map/dot_general | solution.py:436
  258.5 0.0 copy-done.7
  258.5 0.0 copy-start.1
  258.5 14.1 %fusion.24.dg = f32[2048,512]{1,0:T(8,128)} fusion(bf16[4096,2048]{1,0:T(8,128)(2,1)} %get-tuple-element.15, bf16[4096,512]{1,0:T(8,128)(2,1)S(1)} %copy-done.7), kind=kOutput, calls=%fused_computation.36 | convolution fusion | flops 8589934592 | bytes 25165824 | tf_op jit(solution)/shard_map/dot_general | solution.py:434
  272.6 0.0 copy-done
  272.6 0.0 copy-done.1
  272.6 0.0 copy-start.5
  272.6 14.7 %fusion.21.du = f32[2048,512]{1,0:T(8,128)} fusion(bf16[4096,2048]{1,0:T(8,128)(2,1)} %get-tuple-element.15, f32[4096,512]{1,0:T(8,128)S(1)} %fusion.22, bf16[4096,512]{1,0:T(8,128)(2,1)S(1)} %copy-done.1), kind=kOutput, calls=%fused_computation.33 | convolution fusion | flops 8613003264 | bytes 33554432 | tf_op jit(solution)/shard_map/dot_general | solution.py:435
  287.3 0.0 copy-done.5
  287.4 0.0 copy-start.4
  287.4 18.0 %fusion.23 = f32[4096,2048]{1,0:T(8,128)} fusion(bf16[4096,512]{1,0:T(8,128)(2,1)} %get-tuple-element.22, bf16[2048,512]{1,0:T(8,128)(2,1)S(1)} %copy-done.5), kind=kOutput, calls=%fused_computation.35 | convolution fusion | flops 8589934592 | bytes 39845888 | tf_op jit(solution)/shard_map/dot_general | solution.py:433
  305.3 0.0 copy-done.4
  305.3 31.3 %convolution_add_fusion.dxp = f32[4096,2048]{1,0:T(8,128)} fusion(f32[4096,2048]{1,0:T(8,128)} %fusion.23, bf16[2048,512]{1,0:T(8,128)(2,1)S(1)} %copy-done.4, f32[4096,512]{1,0:T(8,128)} %copy-done, bf16[4096,512]{1,0:T(8,128)(2,1)} %get-tuple-element.23), kind=kOutput, calls=%fused_computation.7 | convolution fusion | flops 8621391872 | bytes 81788928 | tf_op jit(solution)/shard_map/dot_general | solution.py:433
  336.7 221.8 %scatter_results.1 = (bf16[512,512]{1,0:T(8,128)(2,1)}, f32[256,4096]{1,0:T(8,128)}, f32[256,4096]{1,0:T(8,128)}, f32[2048,512]{1,0:T(8,128)}, f32[2,2,256,512]{...) custom-call(f32[4096,2048]{1,0:T(8,128)} %convolution_add_fusion.dxp, ...), custom_call_target="tpu_custom_call" | custom-call | tf_op jit(solution)/shard_map/scatter_results/pallas_call | solution.py:400
  558.5 0.0 copy-start.3
  558.5 2.0 copy.13
  560.6 0.0 copy-start.2
  560.6 4.8 copy.14
  565.4 0.0 copy-done.3
  565.4 2.0 copy.15
  567.4 0.0 copy-done.2
  567.4 2.0 copy.16
Async XLA Ops:
  189.8 14.5 %copy-start.6 = (bf16[512,2048]{1,0:T(8,128)(2,1)S(1)}, bf16[512,2048]{1,0:T(8,128)(2,1)}, u32[]{:S(2)}) copy-start(bf16[512,2048]{1,0:T(8,128)(2,1)} %get-tuple-element.14) | copy-start | bytes 6291460
  216.8 55.8 %copy-start = (f32[4096,512]{1,0:T(8,128)}, f32[4096,512]{1,0:T(8,128)S(1)}, u32[]{:S(2)}) copy-start(f32[4096,512]{1,0:T(8,128)S(1)} %fusion.22) | copy-start | bytes 25165828
  241.0 17.5 %copy-start.7 = (bf16[4096,512]{1,0:T(8,128)(2,1)S(1)}, bf16[4096,512]{1,0:T(8,128)(2,1)}, u32[]{:S(2)}) copy-start(bf16[4096,512]{1,0:T(8,128)(2,1)} %get-tuple-element.22) | copy-start | bytes 12582916
  258.5 14.1 %copy-start.1 = (bf16[4096,512]{1,0:T(8,128)(2,1)S(1)}, bf16[4096,512]{1,0:T(8,128)(2,1)}, u32[]{:S(2)}) copy-start(bf16[4096,512]{1,0:T(8,128)(2,1)} %get-tuple-element.23) | copy-start | bytes 12582916
  272.6 14.7 %copy-start.5 = (bf16[2048,512]{1,0:T(8,128)(2,1)S(1)}, bf16[2048,512]{1,0:T(8,128)(2,1)}, u32[]{:S(2)}) copy-start(bf16[2048,512]{1,0:T(8,128)(2,1)} %get-tuple-element.17) | copy-start | bytes 6291460
  287.4 18.0 %copy-start.4 = (bf16[2048,512]{1,0:T(8,128)(2,1)S(1)}, bf16[2048,512]{1,0:T(8,128)(2,1)}, u32[]{:S(2)}) copy-start(bf16[2048,512]{1,0:T(8,128)(2,1)} %get-tuple-element.16) | copy-start | bytes 6291460
  558.5 6.8 %copy-start.3 = (f32[256,4096]{1,0:T(8,128)S(1)}, f32[256,4096]{1,0:T(8,128)}, u32[]{:S(2)}) copy-start(f32[256,4096]{1,0:T(8,128)} %get-tuple-element.30) | copy-start | bytes 12582916
  560.6 6.8 %copy-start.2 = (f32[2048,512]{1,0:T(8,128)S(1)}, f32[2048,512]{1,0:T(8,128)}, u32[]{:S(2)}) copy-start(f32[2048,512]{1,0:T(8,128)} %get-tuple-element.31) | copy-start | bytes 12582916
